TPU v7x, 32 devices: a whole 2x2x4 slice. The times are simulated.
32 devices in a mesh: seq: 8 (over z, y), head: 4 (over x, core).
Axes of the slice: x: 2, y: 2, z: 4, core: 2. Of those that a mesh axis runs over, the one named last changes fastest.
Arguments:
- inputs: bfloat16 [2048, 5120], P('seq', 'head'), may hold values from -6 to 6
- time_step: float32 [80, 2048], P('head', 'seq'), may hold values from 0.01 to 0.3
- decay_rate: float32 [80], P('head'), may hold values from 0.0001 to 1
- input_map: bfloat16 [2048, 128], P('seq'), may hold values from -6 to 6
- output_map: bfloat16 [2048, 128], P('seq'), may hold values from -0.59765625 to 0.59765625
- output_grad: bfloat16 [2048, 5120], P('seq', 'head'), may hold values from -3 to 3
- span_states: float32 [8, 80, 64, 128], P('seq', 'head'), may hold values from -6 to 6
- resets: int32 [8], P('seq'), may hold values from 0 to 4095
Outputs:
- grad_inputs: bfloat16 [2048, 5120], P('seq', 'head')
- grad_input_map: float32 [2048, 128], P('seq')
- grad_rate: float32 [80], P('head')
Inputs may be any that keep to these rules, and one draw needn't show every extreme that they name: `resets`: A value p under 256 means that a document starts at position p of that span; a value of 256 or more means that none starts in it.
All inputs are finite; a program needn't handle non-finite values.
Results may differ from a plain program's by a relative error of at most 0.003.
Values sent between devices are 32-bit elements; how exact they have to be, the bound alone decides.
A program may use at most 64 MiB of HBM per device.

v0:
```python
import jax
import jax.numpy as jnp
from jax import lax
from jax.sharding import PartitionSpec as P

highest = lax.Precision.HIGHEST


def prepare(x_block, step_block, decay_rate, b_block, c_block, grad_block, start_state, reset_at):
    block_len = step_block.shape[1]
    positions = jnp.arange(block_len, dtype=jnp.int32)
    later_doc = positions >= reset_at
    no_reset = reset_at >= block_len
    elapsed = jnp.cumsum(step_block, axis=1)
    log_decay = -decay_rate[:, None] * elapsed
    joined = (later_doc[:, None] == later_doc[None, :]) & (positions[None, :] >= positions[:, None])
    log_gaps = log_decay[:, None, :] - log_decay[:, :, None]
    pair_weight = jnp.where(joined[None], jnp.exp(jnp.where(joined[None], log_gaps, 0.0)), 0.0)
    intersection = jnp.dot(b_block, c_block.T, preferred_element_type=jnp.float32)
    products = jnp.einsum("shp,uhp->hsu", x_block, grad_block, preferred_element_type=jnp.float32)
    mixing = (pair_weight * intersection[None]).astype(jnp.bfloat16)
    pair_terms = pair_weight * products
    paired = pair_terms.astype(jnp.bfloat16)
    dx_inner = jnp.einsum("hsu,uhp->shp", mixing, grad_block, preferred_element_type=jnp.float32)
    db_inner = jnp.einsum("hsu,un->hsn", paired, c_block, preferred_element_type=jnp.float32)
    start_weight = jnp.where(later_doc[None], 0.0, jnp.exp(log_decay))
    end_weight = jnp.where(
        (later_doc | no_reset)[None], jnp.exp(log_decay[:, -1:] - log_decay), 0.0
    )
    carry_gain = jnp.where(no_reset, jnp.exp(log_decay[:, -1]), 0.0)
    c_wide = c_block.astype(jnp.float32)
    grad_wide = grad_block.astype(jnp.float32)
    weighted_c = start_weight[:, :, None] * c_wide[None]
    boundary_grad = jnp.einsum("hun,uhp->hpn", weighted_c, grad_wide, precision=highest)
    state_read = jnp.einsum("uhp,hpn->hun", grad_wide, start_state, precision=highest)
    start_term = jnp.sum(state_read * c_wide[None], axis=2)
    inside_term = jnp.sum(
        pair_terms
        * intersection[None]
        * step_block[:, :, None]
        * (elapsed[:, None, :] - elapsed[:, :, None]),
        axis=(1, 2),
    )
    entry_term = jnp.sum(start_weight * elapsed * start_term, axis=1)
    return (
        carry_gain,
        boundary_grad,
        dx_inner,
        db_inner,
        inside_term + entry_term,
        end_weight,
        elapsed,
    )


def finish(prepared, x_block, step_block, b_block, start_state, carried):
    carry_gain, boundary_grad, dx_inner, db_inner, partial_rate, end_weight, elapsed = prepared
    b_wide = b_block.astype(jnp.float32)
    x_wide = x_block.astype(jnp.float32)
    carried_b = jnp.einsum("sn,hpn->shp", b_wide, carried, precision=highest)
    carried_x = jnp.einsum("shp,hpn->hsn", x_wide, carried, precision=highest)
    step_rows = step_block.T[:, :, None]
    end_rows = end_weight.T[:, :, None]
    grad_x = (step_rows * (dx_inner + end_rows * carried_b)).astype(jnp.bfloat16)
    grad_b = jnp.sum(
        step_block[:, :, None] * (db_inner + end_weight[:, :, None] * carried_x), axis=0
    )
    last_elapsed = elapsed[:, -1]
    leaving_term = jnp.sum(
        end_weight
        * step_block
        * (last_elapsed[:, None] - elapsed)
        * jnp.sum(carried_x * b_wide[None], axis=2),
        axis=1,
    )
    through_term = carry_gain * last_elapsed * jnp.sum(carried * start_state, axis=(1, 2))
    return (grad_x, grad_b, partial_rate + leaving_term + through_term)


def backward_step(running, members):
    grad_piece, gain_piece = members
    return (grad_piece + gain_piece[:, None] * running, running)


def body(inputs, time_step, decay_rate, input_map, output_map, output_grad, span_states, resets):
    length = time_step.shape[1]
    block_count = span_states.shape[0]
    block_len = length // block_count
    head_count = decay_rate.shape[0]
    head_width = inputs.shape[1] // head_count
    number = 0
    x_block = inputs.reshape(block_len, head_count, head_width)
    grad_block = output_grad.reshape(block_len, head_count, head_width)
    step_block = time_step
    b_block = input_map
    prepared = prepare(
        x_block,
        step_block,
        decay_rate,
        b_block,
        output_map,
        grad_block,
        span_states[number],
        resets[number],
    )
    pieces = [(prepared, x_block, step_block, b_block)]
    gain_total = jnp.ones((head_count,), jnp.float32)
    grad_total = jnp.zeros_like(span_states[0])
    for number in reversed(range(block_count)):
        gain_block, grad_block_sum = (pieces[number][0][0], pieces[number][0][1])
        grad_total = grad_block_sum + gain_block[:, None, None] * grad_total
        gain_total = gain_block * gain_total
    seq_count = lax.axis_size("seq")
    entries = grad_total.shape[1] * grad_total.shape[2]
    sliced = grad_total.reshape(head_count, seq_count, entries // seq_count)
    received = lax.all_to_all(sliced, "seq", split_axis=1, concat_axis=1, tiled=True)
    gains = lax.all_gather(gain_total[None], "seq", axis=0, tiled=True)
    ending, exclusive = lax.scan(
        backward_step,
        jnp.zeros_like(received[:, 0]),
        (jnp.transpose(received, (1, 0, 2)), gains),
        reverse=True,
    )
    returned = lax.all_to_all(
        jnp.transpose(exclusive, (1, 0, 2)), "seq", split_axis=1, concat_axis=1, tiled=True
    )
    incoming = returned.reshape(grad_total.shape)
    carried = incoming
    grad_x_list = [None] * block_count
    grad_b_list = [None] * block_count
    rate_total = jnp.zeros((head_count,), jnp.float32)
    for number in reversed(range(block_count)):
        prepared, x_block, step_block, b_block = pieces[number]
        grad_x, grad_b, rate_part = finish(
            prepared, x_block, step_block, b_block, span_states[number], carried
        )
        grad_x_list[number] = grad_x.reshape(block_len, head_count * head_width)
        grad_b_list[number] = grad_b
        rate_total = rate_part
        carried = prepared[1] + prepared[0][:, None, None] * carried
    grad_inputs = grad_x_list[0]
    grad_input_map = lax.psum(grad_b_list[0], "head")
    grad_rate = -lax.psum(rate_total, "seq")
    return (grad_inputs, grad_input_map, grad_rate)


def solution(mesh):
    in_specs = (
        P("seq", "head"),
        P("head", "seq"),
        P("head"),
        P("seq", None),
        P("seq", None),
        P("seq", "head"),
        P("seq", "head", None, None),
        P("seq"),
    )
    out_specs = (P("seq", "head"), P("seq", None), P("head"))
    return jax.shard_map(body, mesh=mesh, in_specs=in_specs, out_specs=out_specs, check_vma=False)
```

profile of v0, /device:TPU:0, one launch (start us, length us, event | category | flops | bytes accessed | tf_op | source)
XLA Modules:
  0.0 141.0 jit_solution(17333116644024165966)
XLA Ops:
  8.6 0.8 reshape.290
  11.2 0.9 copy.37
  12.2 1.4 copy.36
  13.6 1.7 %fusion.31 = f32[20,64,128]{2,1,0:T(8,128)S(1)} fusion(bf16[256,20,64]{0,2,1:T(8,128)(2,1)S(1)} %bitcast.80, f32[256,128]{0,1:T(8,128)S(1)} %copy.37, f32[20,256]{1,0:T(8,128)S(1)} %get-tuple-element.152, f32[20]{0:T(128)S(1)} %broadcast_multiply_fusion.1), kind=kOutput, calls=%fused_computation.38 | convolution fusion | flops 504135680 | bytes 1462352 | tf_op jit(solution)/shard_map/hun,uhp->hpn/dot_general | solution.py:34
  15.4 1.3 copy.39
  16.7 7.3 %all-to-all-start = ((f32[20,8,1024]{2,0,1:T(8,128)}), f32[20,8,1024]{2,0,1:T(8,128)S(1)}, u32[]{:S(2)}, u32[]{:S(2)}) async-start(f32[20,8,1024]{2,0,1:T(8,128)} %copy.39), calls=%async_computation | async-start | bytes 1572864 | tf_op jit(solution)/shard_map/all_to_all | solution.py:116
  25.6 26.1 %all-reduce = f32[160]{0:T(256)S(1)} all-reduce(f32[160]{0:T(256)S(1)} %dynamic-update-slice), channel_id=2, replica_groups=mesh['seq'=8,'head'=4] {'seq'}, use_global_device_ids=true, to_apply=%add | all-reduce | flops 160 | bytes 1280
  53.9 0.7 slice_reduce_fusion.1
  54.7 1.4 %fusion.37 = pred[256,256]{1,0:T(8,128)(4,1)} fusion(pred[256]{0:T(512)(128)(4,1)} %copy-done.10), kind=kLoop, calls=%fused_computation.42 | loop fusion | flops 196608 | bytes 65792 | tf_op jit(solution)/shard_map/and | solution.py:16
  56.1 1.8 %fusion.43 = f32[256,256]{1,0:T(8,128)} fusion(bf16[256,128]{1,0:T(8,128)(2,1)} %param.13, bf16[256,128]{1,0:T(8,128)(2,1)} %param.14), kind=kOutput, calls=%fused_computation.64 | convolution fusion | flops 16777216 | bytes 393216 | tf_op jit(solution)/shard_map/dot_general | solution.py:19
  57.9 1.0 broadcast_in_dim.97
  58.9 11.4 %while.17 = (s32[]{:T(128)}, f32[20,1024]{1,0:T(8,128)S(1)}, f32[8,20,1024]{2,1,0:T(8,128)}, f32[8,20,1024]{2,1,0:T(8,128)S(1)}, f32[8,20]{1,0:T(8,128)}, /*index=5*/s32[]{:T(128)}, s32[]{:T(128)}, s32[]{:T(128)}) while((s32[]{:T(128)}, f32[20,1024]{1,0:T(8,128)S(1)}, f32[8,20,1024]{2,1,0:T(8,128)}, f32[8,20,1024]{2,1,0:T(8,128)S(1)}, ...), condition=%wide.region_3.4_spmd.clone, body=%wide.region_2.3_spmd.clone.sunk | while | flops 81924 | bytes 426352 | solution.py:118
  60.3 0.7 fusion.55
  61.7 0.7 fusion.55
  63.1 0.7 fusion.55
  64.6 0.7 fusion.55
  66.0 0.7 fusion.55
  67.4 0.7 fusion.55
  68.9 0.7 fusion.55
  70.3 4.5 %all-to-all-start.1 = ((f32[20,8,1024]{2,0,1:T(8,128)}), f32[20,8,1024]{2,0,1:T(8,128)S(1)}, u32[]{:S(2)}, u32[]{:S(2)}) async-start(f32[20,8,1024]{2,0,1:T(8,128)} %bitcast.8), calls=%async_computation.1 | async-start | bytes 1572864 | tf_op jit(solution)/shard_map/all_to_all | solution.py:124
  74.8 2.8 %multiply_reduce_fusion.1 = f32[20,256]{1,0:T(8,128)} fusion(bf16[256,20,64]{0,2,1:T(8,128)(2,1)S(1)} %bitcast.81, f32[256,128]{0,1:T(8,128)} %copy-done.7, f32[1,20,64,128]{3,2,1,0:T(8,128)S(1)} %copy-done.2), kind=kOutput, calls=%fused_computation.17 | convolution fusion | flops 504622080 | bytes 1462272 | tf_op jit(solution)/shard_map/uhp,hpn->hun/dot_general | solution.py:35
  77.7 3.7 %fusion.21 = f32[256,20,64]{0,2,1:T(8,128)} fusion(bf16[256,20,64]{0,2,1:T(8,128)(2,1)S(1)} %bitcast.82, f32[256,256]{1,0:T(8,128)} %fusion.43, f32[20,256]{1,0:T(8,128)S(1)} %get-tuple-element.153, pred[256,256]{1,0:T(8,128)(4,1)} %fusion.37), kind=kOutput, calls=%fused_computation.29 | convolution fusion | flops 174325760 | bytes 2314240 | tf_op jit(solution)/shard_map/hsu,uhp->shp/dot_general | solution.py:24
  81.4 5.3 %multiply_reduce_fusion = (f32[20]{0:T(128)}, f32[20,256,256]{2,1,0:T(8,128)}) fusion(f32[20,256]{1,0:T(8,128)S(1)} %bitcast.86, f32[20,256]{1,0:T(8,128)S(1)} %copy-done.6, f32[256,256]{1,0:T(8,128)S(1)} %copy-done.5, f32[20,256]{1,0:T(8,128)S(1)} %get-tuple-element.153, pred[256,256]{1,0:T(8,128)(4,1)S(1)} %copy-done.8, ...), kind=kOutput, calls=%fused_computation.4 | convolution fusion | flops 179568624 | bytes 6942800 | tf_op jit(solution)/shard_map/shp,uhp->hsu/dot_general | solution.py:20
  86.8 5.5 %all-to-all-done.1 = f32[20,8,1024]{2,0,1:T(8,128)S(1)} async-done(((f32[20,8,1024]{2,0,1:T(8,128)}), f32[20,8,1024]{2,0,1:T(8,128)S(1)}, u32[]{:S(2)}, u32[]{:S(2)}) %all-to-all-start.1) | async-done | bytes 655392 | tf_op jit(solution)/shard_map/all_to_all | solution.py:124
  92.3 1.1 multiply_reduce_fusion.2
  93.4 2.8 %fusion.9 = (f32[20,256]{1,0:T(8,128)S(1)}, f32[20,128,256]{1,2,0:T(8,128)S(1)}) fusion(f32[256,128]{1,0:T(8,128)} %convert_element_type.21, f32[20,64,128]{2,1,0:T(8,128)S(1)} %reshape.294, bf16[256,20,64]{0,2,1:T(8,128)(2,1)S(1)} %bitcast.77), kind=kOutput, calls=%fused_computation.16 | convolution fusion | flops 504622080 | bytes 4083712 | tf_op jit(solution)/shard_map/shp,hpn->hsn/dot_general | solution.py:61
  96.5 5.2 %fusion.8 = f32[256,128]{1,0:T(8,128)} fusion(f32[20,128,256]{1,2,0:T(8,128)S(1)} %get-tuple-element.155, f32[20,256]{1,0:T(8,128)S(1)} %get-tuple-element.150, f32[20,256]{1,0:T(8,128)S(1)} %copy-done.6, f32[20,256,256]{2,1,0:T(8,128)} %get-tuple-element.157, f32[20,256]{1,0:T(8,128)S(1)} %get-tuple-element.153, pred[256,256]{1,0:T(8,128)(4,1)} %fusion.37, ...), kind=kOutput, calls=%fused_computation.15 | convolution fusion | flops 344686592 | bytes 8187904 | tf_op jit(solution)/shard_map/hsu,un->hsn/dot_general | solution.py:25
  101.8 0.7 fusion.25
  102.4 19.4 %psum.15 = f32[20]{0:T(128)S(1)} all-reduce(f32[20]{0:T(128)S(1)} %multiply_add_fusion), channel_id=1, replica_groups=mesh['seq'=8,'head'=4] {'seq'}, use_global_device_ids=true, to_apply=%region_12.13 | all-reduce | flops 20 | bytes 160 | tf_op jit(solution)/shard_map/psum | solution.py:143
  121.8 1.1 copy.44
  123.4 9.1 %all-reduce.3.cloned.1.call-done = f32[256,128]{1,0:T(8,128)} async-done(((f32[256,128]{1,0:T(8,128)}), f32[256,128]{1,0:T(8,128)}) %all-reduce.3.cloned.1.call-update) | async-done | bytes 131088 | tf_op jit(solution)/shard_map/psum | solution.py:142
  132.6 1.6 %copy.62 = f32[256,128]{1,0:T(8,128)} copy(f32[256,128]{1,0:T(8,128)} %all-reduce.3.cloned.1.call-done) | data formatting | bytes 262144
  (90 shorter events, 13.1 us)
Async XLA Ops:
  7.2 16.8 %copy-start.20 = (u32[32]{0:T(128)S(1)}, u32[32]{0:T(128)}, u32[]{:S(2)}) copy-start(u32[32]{0:T(128)} %constant.57) | copy-start | bytes 388
  7.2 45.2 %copy-start.3 = (bf16[256,128]{1,0:T(8,128)(2,1)S(1)}, bf16[256,128]{1,0:T(8,128)(2,1)}, u32[]{:S(2)}) copy-start(bf16[256,128]{1,0:T(8,128)(2,1)} %param.13) | copy-start | bytes 196612
  7.2 45.8 %copy-start.1 = (bf16[256,1280]{1,0:T(8,128)(2,1)S(1)}, bf16[256,1280]{1,0:T(8,128)(2,1)}, u32[]{:S(2)}) copy-start(bf16[256,1280]{1,0:T(8,128)(2,1)} %param.10) | copy-start | bytes 1966084
  7.2 46.0 %copy-start.2 = (f32[1,20,64,128]{3,2,1,0:T(8,128)S(1)}, f32[1,20,64,128]{3,2,1,0:T(8,128)}, u32[]{:S(2)}) copy-start(f32[1,20,64,128]{3,2,1,0:T(8,128)} %param.16) | copy-start | bytes 1966084
  8.6 43.7 %copy-start.14 = (f32[20]{0:T(128)}, f32[20]{0:T(128)S(1)}, u32[]{:S(2)}) copy-start(f32[20]{0:T(128)S(1)} %neg.7) | copy-start | bytes 244
  10.9 41.4 %copy-start.10 = (pred[256]{0:T(512)(128)(4,1)}, pred[256]{0:T(512)(128)(4,1)S(1)}, u32[]{:S(2)}) copy-start(pred[256]{0:T(512)(128)(4,1)S(1)} %get-tuple-element.158) | copy-start | bytes 772
  11.2 41.1 %copy-start.11 = (f32[20]{0:T(128)}, f32[20]{0:T(128)S(1)}, u32[]{:S(2)}) copy-start(f32[20]{0:T(128)S(1)} %get-tuple-element.137) | copy-start | bytes 244
  12.2 1.4 copy-start.7
  16.7 41.2 %all-to-all-start = ((f32[20,8,1024]{2,0,1:T(8,128)}), f32[20,8,1024]{2,0,1:T(8,128)S(1)}, u32[]{:S(2)}, u32[]{:S(2)}) async-start(f32[20,8,1024]{2,0,1:T(8,128)} %copy.39), calls=%async_computation | async-start | bytes 1572864 | tf_op jit(solution)/shard_map/all_to_all | solution.py:116
  70.3 22.0 %all-to-all-start.1 = ((f32[20,8,1024]{2,0,1:T(8,128)}), f32[20,8,1024]{2,0,1:T(8,128)S(1)}, u32[]{:S(2)}, u32[]{:S(2)}) async-start(f32[20,8,1024]{2,0,1:T(8,128)} %bitcast.8), calls=%async_computation.1 | async-start | bytes 1572864 | tf_op jit(solution)/shard_map/all_to_all | solution.py:124
  74.8 57.8 %all-reduce.3.cloned.1.call-start = ((), (), s32[]{:S(2)}) async-start(), calls=%async_computation.2 | async-start | bytes 262144 | tf_op jit(solution)/shard_map/psum | solution.py:142
  77.7 3.7 %copy-start.5 = (f32[256,256]{1,0:T(8,128)S(1)}, f32[256,256]{1,0:T(8,128)}, u32[]{:S(2)}) copy-start(f32[256,256]{1,0:T(8,128)} %fusion.43) | copy-start | bytes 786436
  77.7 3.7 %copy-start.6 = (f32[20,256]{1,0:T(8,128)S(1)}, f32[20,256]{1,0:T(8,128)}, u32[]{:S(2)}) copy-start(f32[20,256]{1,0:T(8,128)} %param.11) | copy-start | bytes 61444
  77.7 3.7 %copy-start.8 = (pred[256,256]{1,0:T(8,128)(4,1)S(1)}, pred[256,256]{1,0:T(8,128)(4,1)}, u32[]{:S(2)}) copy-start(pred[256,256]{1,0:T(8,128)(4,1)} %fusion.37) | copy-start | bytes 196612
  86.8 9.4 %copy-start.9 = (f32[20,256]{1,0:T(8,128)S(1)}, f32[20,256]{1,0:T(8,128)}, u32[]{:S(2)}) copy-start(f32[20,256]{1,0:T(8,128)} %multiply_reduce_fusion.1) | copy-start | bytes 61444
  86.8 9.4 %copy-start.12 = (f32[20]{0:T(128)S(1)}, f32[20]{0:T(128)}, u32[]{:S(2)}) copy-start(f32[20]{0:T(128)} %copy-done.11) | copy-start | bytes 244
  86.8 9.5 %copy-start.13 = (f32[20]{0:T(128)S(1)}, f32[20]{0:T(128)}, u32[]{:S(2)}) copy-start(f32[20]{0:T(128)} %slice_reduce_fusion.1) | copy-start | bytes 244
  86.8 9.5 %copy-start.15 = (f32[20]{0:T(128)S(1)}, f32[20]{0:T(128)}, u32[]{:S(2)}) copy-start(f32[20]{0:T(128)} %copy-done.14) | copy-start | bytes 244
  86.8 9.5 %copy-start.16 = (pred[256]{0:T(512)(128)(4,1)S(1)}, pred[256]{0:T(512)(128)(4,1)}, u32[]{:S(2)}) copy-start(pred[256]{0:T(512)(128)(4,1)} %get-tuple-element.159) | copy-start | bytes 772
  86.8 9.5 %copy-start.18 = (pred[256]{0:T(512)(128)(4,1)S(1)}, pred[256]{0:T(512)(128)(4,1)}, u32[]{:S(2)}) copy-start(pred[256]{0:T(512)(128)(4,1)} %compare_bitcast_fusion) | copy-start | bytes 772
  96.5 5.2 %copy-start.17 = (f32[20]{0:T(128)S(1)}, f32[20]{0:T(128)}, u32[]{:S(2)}) copy-start(f32[20]{0:T(128)} %get-tuple-element.148) | copy-start | bytes 244
  96.5 5.2 %copy-start.19 = (f32[20]{0:T(128)S(1)}, f32[20]{0:T(128)}, u32[]{:S(2)}) copy-start(f32[20]{0:T(128)} %get-tuple-element.156) | copy-start | bytes 244
  96.5 5.2 %copy-start = (f32[256,20,64]{0,2,1:T(8,128)S(1)}, f32[256,20,64]{0,2,1:T(8,128)}, u32[]{:S(2)}) copy-start(f32[256,20,64]{0,2,1:T(8,128)} %fusion.21) | copy-start | bytes 3932164
  96.5 5.2 %copy-start.4 = (bf16[256,128]{1,0:T(8,128)(2,1)S(1)}, bf16[256,128]{1,0:T(8,128)(2,1)}, u32[]{:S(2)}) copy-start(bf16[256,128]{1,0:T(8,128)(2,1)} %param.13) | copy-start | bytes 196612
Sparse Core Ops, SparseCore 0:
  101.8 30.7 all-reduce.2
where the time goes:
time: 142 us; the launch traced here: 141 us
  blocking collectives  45.5 us (32%)
  matrix products  24 us (17%)
  local copies, waits for them, and re-layouts  16.6 us (12%)
  between operations  15.8 us (11%)
  waiting for transfers between devices  14.6 us (10%)
  other arithmetic  12.4 us (9%)
  starting transfers between devices  11.9 us (8%)
    unnamed x1, blocking collectives  26.1 us
    psum x1, blocking collectives, body(): grad_rate = -lax.psum(rate_total, 'seq')  19.4 us
    psum x1, waiting for transfers between devices, body(): grad_input_map = lax.psum(grad_b_list[0], 'head')  9.15 us
    all_to_all x1, starting transfers between devices, body(): lax.all_to_all(sliced, 'seq', split_axis=1, concat_axis=1, tiled=True)  7.31 us
    mul x8, local copies, waits for them, and re-layouts, backward_step(): return (grad_piece + gain_piece[:, None] * running, running)  5.48 us
    all_to_all x1, waiting for transfers between devices, body(): lax.all_to_all(jnp.transpose(exclusive, (1, 0, 2)), 'seq', split_axis=1,...  5.48 us
    dot_general x1, matrix products, prepare(): jnp.einsum('shp,uhp->hsu', x_block, grad_block, preferred_element_type=jn...  5.34 us
    unnamed x51, local copies, waits for them, and re-layouts  5.26 us
  transfers between devices with their start and end apart: 3, of which 2 were waited for; matrix products, arithmetic and copies ran while one was open for 15% of the time, Pallas kernels for 0%

commit v1 on v0

--- a/solution.py
+++ b/solution.py
@@ -113,7 +113,10 @@
     seq_count = lax.axis_size("seq")
     entries = grad_total.shape[1] * grad_total.shape[2]
     sliced = grad_total.reshape(head_count, seq_count, entries // seq_count)
-    received = lax.all_to_all(sliced, "seq", split_axis=1, concat_axis=1, tiled=True)
+    received = jnp.concatenate(
+        lax.all_to_all(jnp.stack(jnp.split(sliced, lax.axis_size("seq"), axis=1)), "seq", 0, 0),
+        axis=1,
+    )
     gains = lax.all_gather(gain_total[None], "seq", axis=0, tiled=True)
     ending, exclusive = lax.scan(
         backward_step,

time: 142 us -> 135 us (0.951)
  blocking collectives: 45.5 us -> 43.5 us
    unnamed x51 -> x56, local copies, waits for them, and re-layouts: 5.26 us -> 10.9 us
    mul x8, local copies, waits for them, and re-layouts: 5.48 us -> 0.06 us  [backward_step(): return (grad_piece + gain_piece[:, None] * running, running)]
    unnamed x1, blocking collectives: 26.1 us -> 24.1 us
where the time goes in v1:
time: 135 us
  blocking collectives  43.5 us (32%)
  matrix products  23.4 us (17%)
  between operations  15.8 us (12%)
  local copies, waits for them, and re-layouts  15.2 us (11%)
  waiting for transfers between devices  13.5 us (10%)
  other arithmetic  11.9 us (9%)
  starting transfers between devices  11.1 us (8%)
    unnamed x1, blocking collectives  24.1 us
    psum x1, blocking collectives, body(): grad_rate = -lax.psum(rate_total, 'seq')  19.4 us
    unnamed x56, local copies, waits for them, and re-layouts  10.9 us
    psum x1, waiting for transfers between devices, body(): grad_input_map = lax.psum(grad_b_list[0], 'head')  9.15 us
    all_to_all x1, starting transfers between devices, body(): lax.all_to_all(jnp.stack(jnp.split(sliced, lax.axis_size('seq'), axis=1))...  7.31 us
    dot_general x1, matrix products, prepare(): jnp.einsum('shp,uhp->hsu', x_block, grad_block, preferred_element_type=jn...  6.15 us
    dynamic_update_slice x8, other arithmetic, body(): lax.scan(backward_step, jnp.zeros_like(received[:, 0]), (jnp.transpose(re...  5.16 us
    dot_general x1, matrix products, prepare(): jnp.einsum('hsu,un->hsn', paired, c_block, preferred_element_type=jnp.flo...  5.16 us
  transfers between devices with their start and end apart: 3, of which 2 were waited for; matrix products, arithmetic and copies ran while one was open for 15% of the time, Pallas kernels for 0%

profile of v1, /device:TPU:0, one launch (start us, length us, event | category | flops | bytes accessed | tf_op | source)
XLA Modules:
  0.0 134.6 jit_solution(3752591402788101955)
XLA Ops:
  8.6 0.8 reshape.296
  10.6 0.9 copy.61
  11.6 1.4 %copy.60 = bf16[256,1280]{0,1:T(8,128)(2,1)S(1)} copy(bf16[256,1280]{1,0:T(8,128)(2,1)} %param.15) | data formatting | bytes 1310720 | tf_op args[5]
  13.0 0.8 copy-done.3
  13.8 1.7 %fusion.31 = f32[20,64,128]{2,1,0:T(8,128)S(1)} fusion(bf16[256,20,64]{0,2,1:T(8,128)(2,1)S(1)} %bitcast.117, f32[256,128]{0,1:T(8,128)S(1)} %copy.61, f32[20,256]{1,0:T(8,128)S(1)} %get-tuple-element.160, f32[20]{0:T(128)S(1)} %broadcast_multiply_fusion.1), kind=kOutput, calls=%fused_computation.38 | convolution fusion | flops 504135680 | bytes 1462352 | tf_op jit(solution)/shard_map/hun,uhp->hpn/dot_general | solution.py:34
  16.3 0.7 fusion.44
  17.0 0.7 fusion.43
  17.7 0.7 fusion.42
  18.4 0.7 fusion.41
  19.1 0.7 fusion.40
  19.8 0.7 fusion.39
  20.5 0.7 fusion.38
  21.2 7.3 %all-to-all-start = ((f32[8,20,1,1024]{3,2,1,0:T(1,128)}), f32[8,20,1,1024]{3,2,1,0:T(1,128)S(1)}, u32[]{:S(2)}, u32[]{:S(2)}) async-start(f32[8,20,1,1024]{3,2,1,0:T(1,128)} %fusion.38), calls=%async_computation | async-start | bytes 1310720 | tf_op jit(solution)/shard_map/all_to_all | solution.py:117
  30.0 24.1 %all-reduce = f32[160]{0:T(256)S(1)} all-reduce(f32[160]{0:T(256)S(1)} %dynamic-update-slice), channel_id=2, replica_groups=mesh['seq'=8,'head'=4] {'seq'}, use_global_device_ids=true, to_apply=%add | all-reduce | flops 160 | bytes 1280
  55.9 0.7 fusion.37
  56.7 0.9 fusion.51
  57.7 1.0 broadcast_in_dim.97
  58.7 6.1 %while.17 = (s32[]{:T(128)}, f32[20,1024]{1,0:T(8,128)S(1)}, f32[8,20,1024]{2,1,0:T(8,128)}, f32[8,20,1024]{2,1,0:T(8,128)S(1)}, f32[8,20]{1,0:T(8,128)S(1)}, /*index=5*/s32[]{:T(128)}, s32[]{:T(128)}, s32[]{:T(128)}) while((s32[]{:T(128)}, f32[20,1024]{1,0:T(8,128)S(1)}, f32[8,20,1024]{2,1,0:T(8,128)}, ...), condition=%wide.region_3.4_spmd.clone, body=%wide.region_2.3_spmd.clone.sunk | while | flops 81924 | bytes 426352 | solution.py:121
  64.8 3.7 %all-to-all-start.1 = ((f32[20,8,1024]{2,0,1:T(8,128)}), f32[20,8,1024]{2,0,1:T(8,128)S(1)}, u32[]{:S(2)}, u32[]{:S(2)}) async-start(f32[20,8,1024]{2,0,1:T(8,128)} %bitcast.19), calls=%async_computation.1 | async-start | bytes 1572864 | tf_op jit(solution)/shard_map/all_to_all | solution.py:127
  68.6 3.0 %multiply_reduce_fusion.1 = f32[20,256]{1,0:T(8,128)} fusion(bf16[256,20,64]{0,2,1:T(8,128)(2,1)} %bitcast.118, f32[256,128]{0,1:T(8,128)} %copy-done.14, f32[1,20,64,128]{3,2,1,0:T(8,128)S(1)} %copy-done.2), kind=kOutput, calls=%fused_computation.17 | convolution fusion | flops 504622080 | bytes 1462272 | tf_op jit(solution)/shard_map/uhp,hpn->hun/dot_general | solution.py:35
  71.6 3.9 %fusion.21 = f32[256,20,64]{0,2,1:T(8,128)} fusion(bf16[256,20,64]{0,2,1:T(8,128)(2,1)} %bitcast.119, f32[256,256]{1,0:T(8,128)S(1)} %copy-done.10, f32[20,256]{1,0:T(8,128)S(1)} %get-tuple-element.161, pred[256,256]{1,0:T(8,128)(4,1)S(1)} %copy-done.15), kind=kOutput, calls=%fused_computation.29 | convolution fusion | flops 174325760 | bytes 2314240 | tf_op jit(solution)/shard_map/hsu,uhp->shp/dot_general | solution.py:24
  75.6 6.2 %multiply_reduce_fusion = (f32[20]{0:T(128)}, f32[20,256,256]{2,1,0:T(8,128)}) fusion(f32[20,256]{1,0:T(8,128)S(1)} %bitcast.124, f32[20,256]{1,0:T(8,128)S(1)} %copy-done.12, f32[256,256]{1,0:T(8,128)S(1)} %copy-done.10, f32[20,256]{1,0:T(8,128)} %copy-done.16, pred[256,256]{1,0:T(8,128)(4,1)S(1)} %copy-done.15, bf16[256,20,64]{0,2,1:T(8,128)(2,1)S(1)} %bitcast.113, ...), kind=kOutput, calls=%fused_computation.4 | convolution fusion | flops 179568624 | bytes 6942800 | tf_op jit(solution)/shard_map/shp,uhp->hsu/dot_general | solution.py:20
  81.7 4.3 %all-to-all-done.1 = f32[20,8,1024]{2,0,1:T(8,128)S(1)} async-done(((f32[20,8,1024]{2,0,1:T(8,128)}), f32[20,8,1024]{2,0,1:T(8,128)S(1)}, u32[]{:S(2)}, u32[]{:S(2)}) %all-to-all-start.1) | async-done | bytes 655392 | tf_op jit(solution)/shard_map/all_to_all | solution.py:127
  86.0 1.1 multiply_reduce_fusion.2
  87.2 1.9 %fusion.9 = (f32[20,256]{1,0:T(8,128)S(1)}, f32[20,128,256]{1,2,0:T(8,128)S(1)}) fusion(f32[256,128]{1,0:T(8,128)S(1)} %copy-done.7, f32[20,64,128]{2,1,0:T(8,128)S(1)} %reshape.302, bf16[256,20,64]{0,2,1:T(8,128)(2,1)S(1)} %bitcast.114), kind=kOutput, calls=%fused_computation.16 | convolution fusion | flops 504622080 | bytes 4083712 | tf_op jit(solution)/shard_map/shp,hpn->hsn/dot_general | solution.py:61
  89.1 1.0 multiply_reduce_fusion.4
  90.1 5.2 %fusion.8 = f32[256,128]{1,0:T(8,128)} fusion(f32[20,128,256]{1,2,0:T(8,128)S(1)} %get-tuple-element.163, f32[20,256]{1,0:T(8,128)S(1)} %get-tuple-element.158, f32[20,256]{1,0:T(8,128)} %param.11, f32[20,256,256]{2,1,0:T(8,128)} %get-tuple-element.165, f32[20,256]{1,0:T(8,128)} %copy-done.16, pred[256,256]{1,0:T(8,128)(4,1)} %fusion.37, ...), kind=kOutput, calls=%fused_computation.15 | convolution fusion | flops 344686592 | bytes 8187904 | tf_op jit(solution)/shard_map/hsu,un->hsn/dot_general | solution.py:25
  95.4 0.7 fusion.25
  96.1 19.4 %psum.15 = f32[20]{0:T(128)S(1)} all-reduce(f32[20]{0:T(128)S(1)} %multiply_add_fusion), channel_id=1, replica_groups=mesh['seq'=8,'head'=4] {'seq'}, use_global_device_ids=true, to_apply=%region_12.13 | all-reduce | flops 20 | bytes 160 | tf_op jit(solution)/shard_map/psum | solution.py:146
  115.5 1.1 copy.69
  117.0 9.1 %all-reduce.3.cloned.1.call-done = f32[256,128]{1,0:T(8,128)} async-done(((f32[256,128]{1,0:T(8,128)}), f32[256,128]{1,0:T(8,128)}) %all-reduce.3.cloned.1.call-update) | async-done | bytes 131088 | tf_op jit(solution)/shard_map/psum | solution.py:145
  126.2 1.6 %copy.97 = f32[256,128]{1,0:T(8,128)} copy(f32[256,128]{1,0:T(8,128)} %all-reduce.3.cloned.1.call-done) | data formatting | bytes 262144
  (96 shorter events, 12.0 us)
Async XLA Ops:
  7.2 21.4 %copy-start.19 = (u32[32]{0:T(128)S(1)}, u32[32]{0:T(128)}, u32[]{:S(2)}) copy-start(u32[32]{0:T(128)} %constant.57) | copy-start | bytes 388
  7.2 47.0 %copy-start.5 = (bf16[256,128]{1,0:T(8,128)(2,1)S(1)}, bf16[256,128]{1,0:T(8,128)(2,1)}, u32[]{:S(2)}) copy-start(bf16[256,128]{1,0:T(8,128)(2,1)} %param.13) | copy-start | bytes 196612
  7.2 47.7 %copy-start.1 = (bf16[256,1280]{1,0:T(8,128)(2,1)S(1)}, bf16[256,1280]{1,0:T(8,128)(2,1)}, u32[]{:S(2)}) copy-start(bf16[256,1280]{1,0:T(8,128)(2,1)} %param.10) | copy-start | bytes 1966084
  7.2 47.9 %copy-start.2 = (f32[1,20,64,128]{3,2,1,0:T(8,128)S(1)}, f32[1,20,64,128]{3,2,1,0:T(8,128)}, u32[]{:S(2)}) copy-start(f32[1,20,64,128]{3,2,1,0:T(8,128)} %param.16) | copy-start | bytes 1966084
  10.3 47.2 %copy-start.8 = (f32[3,8,2,128]{3,1,2,0:T(8,128)}, f32[3,8,2,128]{3,1,2,0:T(8,128)S(1)}, u32[]{:S(2)}) copy-start(f32[3,8,2,128]{3,1,2,0:T(8,128)S(1)} %copy.73) | copy-start | bytes 73732
  10.3 46.3 %copy-start.11 = (bf16[256,128]{1,0:T(8,128)(2,1)S(1)}, bf16[256,128]{1,0:T(8,128)(2,1)}, u32[]{:S(2)}) copy-start(bf16[256,128]{1,0:T(8,128)(2,1)} %param.14) | copy-start | bytes 196612
  10.4 61.2 %copy-start.16 = (f32[20,256]{1,0:T(8,128)}, f32[20,256]{1,0:T(8,128)S(1)}, u32[]{:S(2)}) copy-start(f32[20,256]{1,0:T(8,128)S(1)} %get-tuple-element.161) | copy-start | bytes 61444
  11.6 9.6 %copy-start.14 = (f32[256,128]{0,1:T(8,128)}, f32[256,128]{0,1:T(8,128)S(1)}, u32[]{:S(2)}) copy-start(f32[256,128]{0,1:T(8,128)S(1)} %copy.61) | copy-start | bytes 393220
  13.0 0.8 copy-start.3
  21.2 36.3 %all-to-all-start = ((f32[8,20,1,1024]{3,2,1,0:T(1,128)}), f32[8,20,1,1024]{3,2,1,0:T(1,128)S(1)}, u32[]{:S(2)}, u32[]{:S(2)}) async-start(f32[8,20,1,1024]{3,2,1,0:T(1,128)} %fusion.38), calls=%async_computation | async-start | bytes 1310720 | tf_op jit(solution)/shard_map/all_to_all | solution.py:117
  57.7 13.9 %copy-start.10 = (f32[256,256]{1,0:T(8,128)S(1)}, f32[256,256]{1,0:T(8,128)}, u32[]{:S(2)}) copy-start(f32[256,256]{1,0:T(8,128)} %fusion.51) | copy-start | bytes 786436
  57.7 13.9 %copy-start.15 = (pred[256,256]{1,0:T(8,128)(4,1)S(1)}, pred[256,256]{1,0:T(8,128)(4,1)}, u32[]{:S(2)}) copy-start(pred[256,256]{1,0:T(8,128)(4,1)} %fusion.37) | copy-start | bytes 196612
  64.8 21.3 %all-to-all-start.1 = ((f32[20,8,1024]{2,0,1:T(8,128)}), f32[20,8,1024]{2,0,1:T(8,128)S(1)}, u32[]{:S(2)}, u32[]{:S(2)}) async-start(f32[20,8,1024]{2,0,1:T(8,128)} %bitcast.19), calls=%async_computation.1 | async-start | bytes 1572864 | tf_op jit(solution)/shard_map/all_to_all | solution.py:127
  68.5 57.7 %all-reduce.3.cloned.1.call-start = ((), (), s32[]{:S(2)}) async-start(), calls=%async_computation.2 | async-start | bytes 262144 | tf_op jit(solution)/shard_map/psum | solution.py:145
  71.6 3.9 %copy-start.4 = (bf16[256,1280]{0,1:T(8,128)(2,1)S(1)}, bf16[256,1280]{0,1:T(8,128)(2,1)}, u32[]{:S(2)}) copy-start(bf16[256,1280]{0,1:T(8,128)(2,1)} %copy-done.3) | copy-start | bytes 1966084
  71.6 3.9 %copy-start.9 = (f32[3,8,2,128]{3,1,2,0:T(8,128)S(1)}, f32[3,8,2,128]{3,1,2,0:T(8,128)}, u32[]{:S(2)}) copy-start(f32[3,8,2,128]{3,1,2,0:T(8,128)} %copy-done.8) | copy-start | bytes 73732
  71.6 3.9 %copy-start.12 = (f32[20,256]{1,0:T(8,128)S(1)}, f32[20,256]{1,0:T(8,128)}, u32[]{:S(2)}) copy-start(f32[20,256]{1,0:T(8,128)} %param.11) | copy-start | bytes 61444
  75.5 11.6 %copy-start.7 = (f32[256,128]{1,0:T(8,128)S(1)}, f32[256,128]{1,0:T(8,128)}, u32[]{:S(2)}) copy-start(f32[256,128]{1,0:T(8,128)} %convert_element_type.21) | copy-start | bytes 393220
  90.1 5.2 %copy-start.17 = (f32[20]{0:T(128)S(1)}, f32[20]{0:T(128)}, u32[]{:S(2)}) copy-start(f32[20]{0:T(128)} %get-tuple-element.156) | copy-start | bytes 244
  90.1 5.2 %copy-start.18 = (f32[20]{0:T(128)S(1)}, f32[20]{0:T(128)}, u32[]{:S(2)}) copy-start(f32[20]{0:T(128)} %get-tuple-element.164) | copy-start | bytes 244
  90.1 5.3 %copy-start = (f32[256,20,64]{0,2,1:T(8,128)S(1)}, f32[256,20,64]{0,2,1:T(8,128)}, u32[]{:S(2)}) copy-start(f32[256,20,64]{0,2,1:T(8,128)} %fusion.21) | copy-start | bytes 3932164
  90.1 5.3 %copy-start.6 = (bf16[256,128]{1,0:T(8,128)(2,1)S(1)}, bf16[256,128]{1,0:T(8,128)(2,1)}, u32[]{:S(2)}) copy-start(bf16[256,128]{1,0:T(8,128)(2,1)} %param.13) | copy-start | bytes 196612
  90.1 5.3 %copy-start.13 = (f32[20,256]{1,0:T(8,128)S(1)}, f32[20,256]{1,0:T(8,128)}, u32[]{:S(2)}) copy-start(f32[20,256]{1,0:T(8,128)} %param.11) | copy-start | bytes 61444
Sparse Core Ops, SparseCore 0:
  95.4 30.7 all-reduce.2
